TPU v7x, 32 devices: a whole 2x2x4 slice. The times are simulated.
32 devices in a mesh: row: 4 (over y, core), col: 8 (over z, x).
Axes of the slice: x: 2, y: 2, z: 4, core: 2. Of those that a mesh axis runs over, the one named last changes fastest.
Arguments:
- sources: bfloat16 [4, 8, 4, 256, 256], P('row', 'col'), may hold values from -6 to 6
- history: bfloat16 [4, 8, 8, 256, 256], P(None, 'col'), may hold values from -4 to 4
- inverse_diagonal: float32 [4, 8, 256], P('row', 'col'), may hold values from 0.3 to 0.6
- far_cores: bfloat16 [4, 8, 32, 4, 8, 8, 32], P('row', None, None, None, 'col'), may hold values from -0.09375 to 0.09375
- target_basis: bfloat16 [4, 8, 256, 32], P('row', 'col'), may hold values from -1 to 1
- source_basis: bfloat16 [4, 8, 256, 32], P(None, 'col'), may hold values from -0.375 to 0.375
- near_blocks: bfloat16 [4, 8, 3, 256, 8, 256], P('row', 'col'), may hold values from -0.078125 to 0.078125
- near_tile: int32 [4, 8, 3], P('row', 'col'), may hold values from 0 to 3
- near_count: int32 [4, 8], P('row', 'col'), may hold values from 1 to 3, as said below
Outputs:
- new_steps: bfloat16 [4, 8, 4, 256, 256], P('row', 'col')
- energies: float32 [4, 256], replicated
Inputs may be any that keep to these rules, and one draw needn't show every extreme that they name: Only slots below near_count are used; in every draw some tile has all 3 slots live.
All inputs are finite; a program needn't handle non-finite values.
Results may differ from a plain program's by a relative error of at most 0.011.
Values may be sent and summed in bfloat16 or wider, within the bound.
A program may use at most 192 MiB of HBM per device.

v0:
```python
import jax
import jax.numpy as jnp
from jax import lax
from jax.sharding import PartitionSpec as P


def local(
    sources,
    history,
    inverse_diagonal,
    far_cores,
    target_basis,
    source_basis,
    near_blocks,
    near_tile,
    near_count,
):
    row_count = history.shape[0]
    col_count = far_cores.shape[1]
    rank_size = far_cores.shape[2]
    lag_count = history.shape[2]
    tile_size = history.shape[3]
    field_count = history.shape[4]
    step_count = sources.shape[2]
    panel_total = row_count * col_count * tile_size
    column_past = history[:, 0]
    basis = source_basis[:, 0]
    projected = jnp.einsum(
        "pta,pktx->pkax", basis, column_past, preferred_element_type=jnp.float32
    ).astype(jnp.bfloat16)
    core_matrix = far_cores.reshape(col_count * rank_size, row_count * lag_count * rank_size)
    own_basis = target_basis[0, 0]
    scaling = inverse_diagonal[0, 0][:, None]
    blocks_here = near_blocks[0, 0]
    tiles_here = near_tile[0, 0]
    live_count = near_count[0, 0]
    outputs = []
    energy_rows = []
    for moment in range(step_count):
        partial_value = jnp.dot(
            core_matrix,
            projected.reshape(row_count * lag_count * rank_size, field_count),
            preferred_element_type=jnp.float32,
        )

        def add_block(slot, total):
            source = lax.dynamic_index_in_dim(
                column_past, tiles_here[slot], 0, keepdims=False
            ).reshape(lag_count * tile_size, field_count)
            block = lax.dynamic_index_in_dim(blocks_here, slot, 0, keepdims=False).reshape(
                tile_size, lag_count * tile_size
            )
            return total + jnp.dot(block, source, preferred_element_type=jnp.float32)

        near = lax.fori_loop(
            0, live_count, add_block, jnp.zeros((tile_size, field_count), jnp.float32)
        )
        own_core = lax.psum_scatter(
            partial_value.astype(jnp.bfloat16), "col", scatter_dimension=0, tiled=True
        )
        far = jnp.dot(own_basis, own_core, preferred_element_type=jnp.float32)
        fresh = (scaling * (sources[0, 0, moment].astype(jnp.float32) - far - near)).astype(
            jnp.bfloat16
        )
        outputs.append(fresh)
        squares = jnp.sum(jnp.square(fresh.astype(jnp.float32)), axis=0) / panel_total
        energy_rows.append(lax.psum(squares, ("row", "col")))
        if moment + 1 < step_count:
            gathered = lax.all_gather(fresh[None], "row", axis=0, tiled=True)
            column_past = jnp.concatenate([gathered[:, None], column_past[:, :-1]], axis=1)
            fresh_proj = jnp.einsum(
                "pta,ptx->pax", basis, gathered, preferred_element_type=jnp.float32
            ).astype(jnp.bfloat16)
            projected = jnp.concatenate([fresh_proj[:, None], projected[:, :-1]], axis=1)
    energies = jnp.stack(energy_rows, axis=0)
    new_steps = jnp.stack(outputs, axis=0)[None, None]
    return (new_steps, energies)


def solution(mesh):
    placed = (
        P("row", "col", None, None, None),
        P(None, "col", None, None, None),
        P("row", "col", None),
        P("row", None, None, None, "col", None, None),
        P("row", "col", None, None),
        P(None, "col", None, None),
        P("row", "col", None, None, None, None),
        P("row", "col", None),
        P("row", "col"),
    )
    return jax.shard_map(
        local,
        mesh=mesh,
        in_specs=placed,
        out_specs=(P("row", "col", None, None, None), P()),
        check_vma=False,
    )
```

profile of v0, /device:TPU:0, one launch (start us, length us, event | category | flops | bytes accessed | tf_op | source)
XLA Modules:
  0.0 396.4 jit_solution(5392760271177488294)
XLA Ops:
  7.2 3.5 reshape.69
  10.8 3.2 convolution_convert_fusion
  14.4 0.8 copy.20
  15.2 2.6 copy.29
  17.9 14.3 %while.40 = (s32[]{:T(128)}, f32[256,256]{1,0:T(8,128)S(1)}, s32[]{:T(128)}, bf16[3,256,8,256]{3,1,2,0:T(8,128)(2,1)S(1)}, s32[3]{0:T(128)S(1)}, /*index=5*/bf16...) while((s32[]{:T(128)}, f32[256,256]{1,0:T(8,128)S(1)}, s32[]{:T(128)}, ...), condition=%wide.region_2.3_spmd, body=%wide.region_1.2_spmd.sunk | while | flops 268500992 | bytes 2621629 | solution.py:55
  20.7 1.7 fusion.89
  25.3 1.7 fusion.89
  29.9 1.7 fusion.89
  32.2 4.3 %slice.41 = bf16[4,7,256,256]{3,2,1,0:T(8,128)(2,1)} slice(bf16[4,8,256,256]{3,2,1,0:T(8,128)(2,1)} %get-tuple-element.477), slice={[0:4], [0:7], [0:256], [0:256]} | slice | bytes 7340032 | tf_op jit(solution)/shard_map/slice | solution.py:70
  36.5 1.9 slice.40
  38.4 41.5 %reduce-scatter.13.cloned.1.call-done = bf16[32,256]{1,0:T(8,128)(2,1)} async-done(((bf16[256,256]{1,0:T(8,128)(2,1)}), bf16[32,256]{1,0:T(8,128)(2,1)}) %reduce-scatter.13.cloned.1.call-update) | async-done | bytes 16400
  79.9 1.7 multiply_reduce_fusion.3
  81.6 0.6 copy-done.6
  82.3 7.1 %all-gather = bf16[1024,256]{1,0:T(8,128)(2,1)S(1)} all-gather(bf16[256,256]{1,0:T(8,128)(2,1)S(1)} %get-tuple-element.197), channel_id=2, replica_groups=mesh['row'=4,'col'=8] {'row'}, dimensions={0}, use_global_device_ids=true | all-gather | bytes 655360 | tf_op jit(solution)/shard_map/all_gather | solution.py:69
  89.4 4.5 %pad_maximum_fusion = bf16[4,8,256,256]{3,2,1,0:T(8,128)(2,1)} fusion(bf16[4,1,256,256]{3,2,1,0:T(8,128)(2,1)S(1)} %bitcast.237, bf16[4,7,256,256]{3,2,1,0:T(8,128)(2,1)} %slice.41), kind=kLoop, calls=%fused_computation.29 | loop fusion | flops 2097152 | bytes 8388608 | tf_op jit(solution)/shard_map/concatenate | solution.py:70
  94.0 15.9 %while.41 = (s32[]{:T(128)}, f32[256,256]{1,0:T(8,128)S(1)}, s32[]{:T(128)}, bf16[3,256,8,256]{3,1,2,0:T(8,128)(2,1)S(1)}, s32[3]{0:T(128)S(1)}, /*index=5*/bf16...) while((s32[]{:T(128)}, f32[256,256]{1,0:T(8,128)S(1)}, s32[]{:T(128)}, ...), condition=%wide.region_5.6_spmd, body=%wide.region_4.5_spmd.sunk | while | flops 268500992 | bytes 2621629 | solution.py:55
  94.6 0.7 dynamic_slice.87
  97.4 1.7 fusion.92
  99.7 0.7 dynamic_slice.87
  102.5 1.7 fusion.92
  104.8 0.7 dynamic_slice.87
  107.6 1.7 fusion.92
  110.4 1.2 fusion.46
  111.6 1.1 pad_maximum_fusion.3
  112.7 2.0 fusion.43
  114.8 1.7 copy.22
  116.5 1.2 broadcast_multiply_fusion.3
  117.7 1.8 fusion.50
  119.5 3.5 fusion.25
  123.0 53.8 %reduce-scatter.15.cloned.1.call-done = bf16[32,256]{1,0:T(8,128)(2,1)} async-done(((bf16[256,256]{1,0:T(8,128)(2,1)}), bf16[32,256]{1,0:T(8,128)(2,1)}) %reduce-scatter.15.cloned.1.call-update) | async-done | bytes 16400
  176.8 1.7 multiply_reduce_fusion.2
  178.5 0.6 copy-done.7
  179.2 7.1 %all-gather.1 = bf16[1024,256]{1,0:T(8,128)(2,1)S(1)} all-gather(bf16[256,256]{1,0:T(8,128)(2,1)S(1)} %get-tuple-element.195), channel_id=3, replica_groups=mesh['row'=4,'col'=8] {'row'}, dimensions={0}, use_global_device_ids=true | all-gather | bytes 655360 | tf_op jit(solution)/shard_map/all_gather | solution.py:69
  186.3 4.5 %pad_maximum_fusion.1 = bf16[4,8,256,256]{3,2,1,0:T(8,128)(2,1)} fusion(bf16[4,1,256,256]{3,2,1,0:T(8,128)(2,1)S(1)} %bitcast.240, bf16[4,7,256,256]{3,2,1,0:T(8,128)(2,1)} %fusion.25), kind=kLoop, calls=%fused_computation.31 | loop fusion | flops 2097152 | bytes 8388608 | tf_op jit(solution)/shard_map/concatenate | solution.py:70
  190.9 15.8 %while.42 = (s32[]{:T(128)}, f32[256,256]{1,0:T(8,128)S(1)}, s32[]{:T(128)}, bf16[3,256,8,256]{3,1,2,0:T(8,128)(2,1)S(1)}, s32[3]{0:T(128)S(1)}, /*index=5*/bf16...) while((s32[]{:T(128)}, f32[256,256]{1,0:T(8,128)S(1)}, s32[]{:T(128)}, ...), condition=%wide.region_8.9_spmd, body=%wide.region_7.8_spmd.sunk | while | flops 268500992 | bytes 2621629 | solution.py:55
  191.5 0.7 dynamic_slice.90
  194.2 1.7 fusion.95
  196.6 0.7 dynamic_slice.90
  199.3 1.7 fusion.95
  201.6 0.7 dynamic_slice.90
  204.3 1.7 fusion.95
  206.6 1.2 fusion.47
  207.9 1.1 pad_maximum_fusion.4
  209.0 2.0 fusion.44
  211.0 1.7 copy.24
  212.7 1.2 broadcast_multiply_fusion.2
  214.0 1.8 fusion.49
  215.8 3.4 fusion.24
  219.2 53.8 %reduce-scatter.17.cloned.1.call-done = bf16[32,256]{1,0:T(8,128)(2,1)} async-done(((bf16[256,256]{1,0:T(8,128)(2,1)}), bf16[32,256]{1,0:T(8,128)(2,1)}) %reduce-scatter.17.cloned.1.call-update) | async-done | bytes 16400
  273.0 1.2 multiply_reduce_fusion.1
  274.2 7.1 %all-gather.2 = bf16[1024,256]{1,0:T(8,128)(2,1)S(1)} all-gather(bf16[256,256]{1,0:T(8,128)(2,1)S(1)} %get-tuple-element.193), channel_id=4, replica_groups=mesh['row'=4,'col'=8] {'row'}, dimensions={0}, use_global_device_ids=true | all-gather | bytes 655360 | tf_op jit(solution)/shard_map/all_gather | solution.py:69
  281.4 0.8 copy-done.5
  282.4 1.1 pad_maximum_fusion.5
  283.4 1.4 fusion.45
  284.8 0.8 copy.26
  285.6 4.5 %pad_maximum_fusion.2 = bf16[4,8,256,256]{3,2,1,0:T(8,128)(2,1)} fusion(bf16[4,7,256,256]{3,2,1,0:T(8,128)(2,1)} %fusion.24, bf16[4,1,256,256]{3,2,1,0:T(8,128)(2,1)} %bitcast.246), kind=kLoop, calls=%fused_computation.32 | loop fusion | flops 2097152 | bytes 8388608 | tf_op jit(solution)/shard_map/concatenate | solution.py:70
  290.1 15.3 %while.43 = (s32[]{:T(128)}, f32[256,256]{1,0:T(8,128)S(1)}, s32[]{:T(128)}, bf16[3,256,8,256]{3,1,2,0:T(8,128)(2,1)S(1)}, s32[3]{0:T(128)S(1)}, /*index=5*/bf16...) while((s32[]{:T(128)}, f32[256,256]{1,0:T(8,128)S(1)}, s32[]{:T(128)}, ...), condition=%wide.region_11.12_spmd, body=%wide.region_10.11_spmd.sunk | while | flops 268500992 | bytes 2621629 | solution.py:55
  293.3 1.7 fusion.98
  298.2 1.7 fusion.98
  303.1 1.7 fusion.98
  305.5 40.5 %reduce-scatter.19.cloned.1.call-done = bf16[32,256]{1,0:T(8,128)(2,1)} async-done(((bf16[256,256]{1,0:T(8,128)(2,1)}), bf16[32,256]{1,0:T(8,128)(2,1)}) %reduce-scatter.19.cloned.1.call-update) | async-done | bytes 16400
  346.0 1.2 multiply_reduce_fusion
  347.2 40.1 %all-reduce = (f32[1,256]{1,0:T(1,128)S(1)}, f32[1,256]{1,0:T(1,128)S(1)}, f32[1,256]{1,0:T(1,128)S(1)}, f32[1,256]{1,0:T(1,128)S(1)}) all-reduce(f32[1,256]{1,0:T(1,128)S(1)} %bitcast.261, f32[1,256]{1,0:T(1,128)S(1)} %bitcast.260, f32[1,256]{1,0:T(1,128)S(1)} %bitcast.259, ...), channel_id=1, replica_groups=mesh['row'=4,'col'=8] {'row','col'}, use_global_device_ids=true, to_apply=%region_19.20 | all-reduce | flops 1024 | bytes 8192 | tf_op jit(solution)/shard_map/psum | solution.py:67
  388.0 1.9 maximum_bitcast_fusion
  (58 shorter events, 5.5 us)
Async XLA Ops:
  7.2 3.6 copy-start
  7.2 72.7 %reduce-scatter.13.cloned.1.call-start = ((), (), s32[]{:S(2)}) async-start(), calls=%async_computation.4 | async-start | bytes 147456
  10.8 4.4 %copy-start.1 = (bf16[256,1024]{1,0:T(8,128)(2,1)}, bf16[256,1024]{1,0:T(8,128)(2,1)S(1)}, u32[]{:S(2)}) copy-start(bf16[256,1024]{1,0:T(8,128)(2,1)S(1)} %reshape.69) | copy-start | bytes 1572868
  14.0 1.2 copy-start.4
  14.0 3.9 copy-start.15
  15.2 161.6 %reduce-scatter.15.cloned.1.call-start = ((), (), s32[]{:S(2)}) async-start(), calls=%async_computation.5 | async-start | bytes 147456
  32.2 47.6 %copy-start.9 = (bf16[1,1,256,32]{2,3,1,0:T(8,128)(2,1)S(1)}, bf16[1,1,256,32]{2,3,1,0:T(8,128)(2,1)}, u32[]{:S(2)}) copy-start(bf16[1,1,256,32]{2,3,1,0:T(8,128)(2,1)} %param.21) | copy-start | bytes 49156
  32.2 47.6 %copy-start.10 = (f32[1,1,256]{2,1,0:T(1,128)S(1)}, f32[1,1,256]{2,1,0:T(1,128)}, u32[]{:S(2)}) copy-start(f32[1,1,256]{2,1,0:T(1,128)} %param.19) | copy-start | bytes 3076
  81.6 0.6 copy-start.6
  89.4 4.5 %copy-start.2 = (bf16[1024,256]{1,0:T(8,128)(2,1)}, bf16[1024,256]{1,0:T(8,128)(2,1)S(1)}, u32[]{:S(2)}) copy-start(bf16[1024,256]{1,0:T(8,128)(2,1)S(1)} %all-gather) | copy-start | bytes 1572868
  109.9 0.5 copy-start.16
  116.4 156.6 %reduce-scatter.17.cloned.1.call-start = ((), (), s32[]{:S(2)}) async-start(), calls=%async_computation.6 | async-start | bytes 147456
  119.5 57.3 %copy-start.11 = (f32[1,1,256]{2,1,0:T(1,128)S(1)}, f32[1,1,256]{2,1,0:T(1,128)}, u32[]{:S(2)}) copy-start(f32[1,1,256]{2,1,0:T(1,128)} %param.19) | copy-start | bytes 3076
  178.5 0.6 copy-start.7
  186.3 4.5 %copy-start.3 = (bf16[1024,256]{1,0:T(8,128)(2,1)}, bf16[1024,256]{1,0:T(8,128)(2,1)S(1)}, u32[]{:S(2)}) copy-start(bf16[1024,256]{1,0:T(8,128)(2,1)S(1)} %all-gather.1) | copy-start | bytes 1572868
  186.3 4.6 %copy-start.17 = (s32[3]{0:T(128)S(1)}, s32[3]{0:T(128)}, u32[]{:S(2)}) copy-start(s32[3]{0:T(128)} %copy-done.16) | copy-start | bytes 40
  212.7 133.3 %reduce-scatter.19.cloned.1.call-start = ((), (), s32[]{:S(2)}) async-start(), calls=%async_computation.7 | async-start | bytes 147456
  215.8 57.2 %copy-start.12 = (f32[1,1,256]{2,1,0:T(1,128)S(1)}, f32[1,1,256]{2,1,0:T(1,128)}, u32[]{:S(2)}) copy-start(f32[1,1,256]{2,1,0:T(1,128)} %param.19) | copy-start | bytes 3076
  274.2 7.2 %copy-start.8 = (bf16[256,256]{1,0:T(8,128)(2,1)}, bf16[256,256]{1,0:T(8,128)(2,1)S(1)}, u32[]{:S(2)}) copy-start(bf16[256,256]{1,0:T(8,128)(2,1)S(1)} %get-tuple-element.193) | copy-start | bytes 393220
  281.4 0.8 copy-start.5
  285.6 4.5 %copy-start.18 = (s32[3]{0:T(128)S(1)}, s32[3]{0:T(128)}, u32[]{:S(2)}) copy-start(s32[3]{0:T(128)} %copy-done.16) | copy-start | bytes 40
  290.1 57.1 %copy-start.13 = (f32[256]{0:T(256)S(1)}, f32[256]{0:T(256)}, u32[]{:S(2)}) copy-start(f32[256]{0:T(256)} %broadcast_multiply_fusion.3) | copy-start | bytes 3076
  290.1 57.1 %copy-start.14 = (f32[256]{0:T(256)S(1)}, f32[256]{0:T(256)}, u32[]{:S(2)}) copy-start(f32[256]{0:T(256)} %broadcast_multiply_fusion.2) | copy-start | bytes 3076
Sparse Core Ops, SparseCore 0:
  15.3 64.5 reduce-scatter.12
  116.6 60.1 reduce-scatter.14
  212.8 60.1 reduce-scatter.16
  285.7 60.2 reduce-scatter.18
where the time goes:
time: 398 us; the launch traced here: 396 us
  waiting for transfers between devices  190 us (48%)
  blocking collectives  61.5 us (15%)
  matrix products  37.7 us (9%)
  loops' own time  33.8 us (8%)
  other arithmetic  32.2 us (8%)
  local copies, waits for them, and re-layouts  27.2 us (7%)
  between operations  14 us (4%)
    unnamed x8, waiting for transfers between devices  190 us
    psum x1, blocking collectives, local(): energy_rows.append(lax.psum(squares, ('row', 'col')))  40.1 us
    another operation x4, loops' own time, local(): lax.fori_loop(0, live_count, add_block, jnp.zeros((tile_size, field_count...  33.8 us
    all_gather x3, blocking collectives, local(): gathered = lax.all_gather(fresh[None], 'row', axis=0, tiled=True)  21.4 us
    concatenate x5, other arithmetic, local(): jnp.concatenate([gathered[:, None], column_past[:, :-1]], axis=1)  20.4 us
    dot_general x12, matrix products, add_block(): return total + jnp.dot(block, source, preferred_element_type=jnp.float32)  20.1 us
    unnamed x43, local copies, waits for them, and re-layouts  10.1 us
  transfers between devices with their start and end apart: 4, of which 4 were waited for; matrix products, arithmetic and copies ran while one was open for 10% of the time, Pallas kernels for 0%

commit v1 on v0

--- a/solution.py
+++ b/solution.py
@@ -64,7 +64,7 @@
         )
         outputs.append(fresh)
         squares = jnp.sum(jnp.square(fresh.astype(jnp.float32)), axis=0) / panel_total
-        energy_rows.append(lax.psum(squares, ("row", "col")))
+        energy_rows.append(jnp.sum(lax.all_gather(squares, ("row", "col")), axis=0))
         if moment + 1 < step_count:
             gathered = lax.all_gather(fresh[None], "row", axis=0, tiled=True)
             column_past = jnp.concatenate([gathered[:, None], column_past[:, :-1]], axis=1)

time: 398 us -> 467 us (1.17)
  blocking collectives: 61.5 us -> 279 us
  waiting for transfers between devices: 190 us -> 40.2 us
    all_gather x0 -> x4, blocking collectives: none -> 259 us  [local(): energy_rows.append(jnp.sum(lax.all_gather(squares, ('row', 'col')), axis=0))]
    unnamed x8, waiting for transfers between devices: 190 us -> 40.2 us
    psum x1 -> x0, blocking collectives: 40.1 us -> none  [local(): energy_rows.append(lax.psum(squares, ('row', 'col')))]
    unnamed x43 -> x41, local copies, waits for them, and re-layouts: 10.1 us -> 10.2 us
  transfers between devices with their start and end apart: 4 -> 4, of which waited for: 4 -> 1; matrix products, arithmetic and copies ran while one was open for 10% -> 9% of each run, Pallas kernels for 0% -> 0%
where the time goes in v1:
time: 467 us; the launch traced here: 465 us
  blocking collectives  279 us (60%)
  waiting for transfers between devices  40.2 us (9%)
  matrix products  37.6 us (8%)
  loops' own time  33.9 us (7%)
  other arithmetic  31.9 us (7%)
  local copies, waits for them, and re-layouts  27.3 us (6%)
  between operations  14 us (3%)
    all_gather x4, blocking collectives, local(): energy_rows.append(jnp.sum(lax.all_gather(squares, ('row', 'col')), axis=0))  259 us
    unnamed x8, waiting for transfers between devices  40.2 us
    another operation x4, loops' own time, local(): lax.fori_loop(0, live_count, add_block, jnp.zeros((tile_size, field_count...  33.9 us
    all_gather x3, blocking collectives, local(): gathered = lax.all_gather(fresh[None], 'row', axis=0, tiled=True)  20.5 us
    concatenate x5, other arithmetic, local(): jnp.concatenate([gathered[:, None], column_past[:, :-1]], axis=1)  20.4 us
    dot_general x12, matrix products, add_block(): return total + jnp.dot(block, source, preferred_element_type=jnp.float32)  20.1 us
    unnamed x41, local copies, waits for them, and re-layouts  10.2 us
  transfers between devices with their start and end apart: 4, of which 1 were waited for; matrix products, arithmetic and copies ran while one was open for 9% of the time, Pallas kernels for 0%

profile of v1, /device:TPU:0, one launch (start us, length us, event | category | flops | bytes accessed | tf_op | source)
XLA Modules:
  0.0 464.6 jit_solution(12758836999442726398)
XLA Ops:
  7.2 3.5 reshape.105
  10.8 3.2 convolution_convert_fusion
  14.4 0.8 copy.20
  15.2 2.6 copy.29
  17.9 15.7 %while.40 = (s32[]{:T(128)}, f32[256,256]{1,0:T(8,128)S(1)}, s32[]{:T(128)}, bf16[3,256,8,256]{3,1,2,0:T(8,128)(2,1)S(1)}, s32[3]{0:T(128)S(1)}, /*index=5*/bf16...) while((s32[]{:T(128)}, f32[256,256]{1,0:T(8,128)S(1)}, s32[]{:T(128)}, ...), condition=%wide.region_2.3_spmd, body=%wide.region_1.2_spmd.sunk | while | flops 268500992 | bytes 2621629 | solution.py:55
  18.6 0.7 dynamic_slice.84
  21.2 1.7 fusion.89
  23.6 0.7 dynamic_slice.84
  26.2 1.7 fusion.89
  28.6 0.7 dynamic_slice.84
  31.3 1.7 fusion.89
  33.6 4.3 slice.41
  37.9 1.8 slice.40
  39.8 40.1 %reduce-scatter.13.cloned.1.call-done = bf16[32,256]{1,0:T(8,128)(2,1)} async-done(((bf16[256,256]{1,0:T(8,128)(2,1)}), bf16[32,256]{1,0:T(8,128)(2,1)}) %reduce-scatter.13.cloned.1.call-update) | async-done | bytes 16400
  79.9 1.7 multiply_reduce_fusion.3
  81.6 0.7 copy-done.6
  82.3 7.1 %all-gather = bf16[1024,256]{1,0:T(8,128)(2,1)S(1)} all-gather(bf16[256,256]{1,0:T(8,128)(2,1)S(1)} %get-tuple-element.193), channel_id=2, replica_groups=mesh['row'=4,'col'=8] {'row'}, dimensions={0}, use_global_device_ids=true | all-gather | bytes 655360 | tf_op jit(solution)/shard_map/all_gather | solution.py:69
  89.4 4.5 pad_maximum_fusion
  94.0 15.8 %while.41 = (s32[]{:T(128)}, f32[256,256]{1,0:T(8,128)S(1)}, s32[]{:T(128)}, bf16[3,256,8,256]{3,1,2,0:T(8,128)(2,1)S(1)}, s32[3]{0:T(128)S(1)}, /*index=5*/bf16...) while((s32[]{:T(128)}, f32[256,256]{1,0:T(8,128)S(1)}, s32[]{:T(128)}, ...), condition=%wide.region_5.6_spmd, body=%wide.region_4.5_spmd.sunk | while | flops 268500992 | bytes 2621629 | solution.py:55
  94.6 0.7 dynamic_slice.87
  97.3 1.7 fusion.92
  99.7 0.7 dynamic_slice.87
  102.4 1.7 fusion.92
  104.7 0.7 dynamic_slice.87
  107.4 1.7 fusion.92
  110.4 1.2 fusion.46
  111.6 1.1 pad_maximum_fusion.3
  112.7 2.0 fusion.43
  114.7 1.7 copy.22
  116.4 0.7 broadcast_multiply_fusion.3
  117.1 1.8 fusion.50
  119.0 66.1 %all-gather.7 = f32[32,1,256]{2,1,0:T(1,128)S(1)} all-gather(f32[1,1,256]{2,1,0:T(1,128)S(1)} %bitcast.262), channel_id=5, replica_groups=mesh['row'=4,'col'=8] {'row','col'}, dimensions={0}, use_global_device_ids=true | all-gather | bytes 33792 | tf_op jit(solution)/shard_map/all_gather | solution.py:67
  185.6 3.5 fusion.25
  189.2 1.7 multiply_reduce_fusion.2
  190.9 0.6 copy-done.7
  191.6 6.9 %all-gather.1 = bf16[1024,256]{1,0:T(8,128)(2,1)S(1)} all-gather(bf16[256,256]{1,0:T(8,128)(2,1)S(1)} %get-tuple-element.191), channel_id=3, replica_groups=mesh['row'=4,'col'=8] {'row'}, dimensions={0}, use_global_device_ids=true | all-gather | bytes 655360 | tf_op jit(solution)/shard_map/all_gather | solution.py:69
  198.4 4.5 pad_maximum_fusion.1
  203.0 14.5 %while.42 = (s32[]{:T(128)}, f32[256,256]{1,0:T(8,128)S(1)}, s32[]{:T(128)}, bf16[3,256,8,256]{3,1,2,0:T(8,128)(2,1)S(1)}, s32[3]{0:T(128)S(1)}, /*index=5*/bf16...) while((s32[]{:T(128)}, f32[256,256]{1,0:T(8,128)S(1)}, s32[]{:T(128)}, ...), condition=%wide.region_8.9_spmd, body=%wide.region_7.8_spmd.sunk | while | flops 268500992 | bytes 2621629 | solution.py:55
  205.9 1.7 fusion.95
  210.6 1.7 fusion.95
  215.2 1.7 fusion.95
  217.6 1.2 fusion.47
  218.8 1.1 pad_maximum_fusion.4
  219.9 2.0 fusion.44
  221.9 1.7 copy.24
  223.6 0.7 broadcast_multiply_fusion.2
  224.3 1.8 fusion.49
  226.1 63.6 %all-gather.8 = f32[32,1,256]{2,1,0:T(1,128)S(1)} all-gather(f32[1,1,256]{2,1,0:T(1,128)S(1)} %bitcast.263), channel_id=6, replica_groups=mesh['row'=4,'col'=8] {'row','col'}, dimensions={0}, use_global_device_ids=true | all-gather | bytes 33792 | tf_op jit(solution)/shard_map/all_gather | solution.py:67
  289.8 3.4 fusion.24
  293.2 1.2 multiply_reduce_fusion.1
  294.4 6.5 %all-gather.2 = bf16[1024,256]{1,0:T(8,128)(2,1)S(1)} all-gather(bf16[256,256]{1,0:T(8,128)(2,1)S(1)} %get-tuple-element.189), channel_id=4, replica_groups=mesh['row'=4,'col'=8] {'row'}, dimensions={0}, use_global_device_ids=true | all-gather | bytes 655360 | tf_op jit(solution)/shard_map/all_gather | solution.py:69
  300.9 0.8 copy-done.5
  301.9 1.1 pad_maximum_fusion.5
  303.0 1.4 fusion.45
  304.4 0.8 copy.26
  305.2 4.4 pad_maximum_fusion.2
  309.7 15.3 %while.43 = (s32[]{:T(128)}, f32[256,256]{1,0:T(8,128)S(1)}, s32[]{:T(128)}, bf16[3,256,8,256]{3,1,2,0:T(8,128)(2,1)S(1)}, s32[3]{0:T(128)S(1)}, /*index=5*/bf16...) while((s32[]{:T(128)}, f32[256,256]{1,0:T(8,128)S(1)}, s32[]{:T(128)}, ...), condition=%wide.region_11.12_spmd, body=%wide.region_10.11_spmd.sunk | while | flops 268500992 | bytes 2621629 | solution.py:55
  312.9 1.7 fusion.98
  317.8 1.7 fusion.98
  322.6 1.7 fusion.98
  325.0 65.7 %all-gather.9 = f32[32,1,256]{2,1,0:T(1,128)S(1)} all-gather(f32[1,1,256]{2,1,0:T(1,128)S(1)} %bitcast.264), channel_id=7, replica_groups=mesh['row'=4,'col'=8] {'row','col'}, dimensions={0}, use_global_device_ids=true | all-gather | bytes 33792 | tf_op jit(solution)/shard_map/all_gather | solution.py:67
  390.8 1.2 multiply_reduce_fusion
  392.0 63.5 %all-gather.10 = f32[32,1,256]{2,1,0:T(1,128)S(1)} all-gather(f32[1,1,256]{2,1,0:T(1,128)S(1)} %bitcast.265), channel_id=8, replica_groups=mesh['row'=4,'col'=8] {'row','col'}, dimensions={0}, use_global_device_ids=true | all-gather | bytes 33792 | tf_op jit(solution)/shard_map/all_gather | solution.py:67
  456.2 1.9 maximum_bitcast_fusion
  (63 shorter events, 6.4 us)
Async XLA Ops:
  7.2 3.6 copy-start
  7.2 72.7 %reduce-scatter.13.cloned.1.call-start = ((), (), s32[]{:S(2)}) async-start(), calls=%async_computation.4 | async-start | bytes 147456
  10.8 4.4 copy-start.1
  14.0 1.2 copy-start.4
  14.0 3.9 copy-start.14
  15.2 174.0 %reduce-scatter.15.cloned.1.call-start = ((), (), s32[]{:S(2)}) async-start(), calls=%async_computation.5 | async-start | bytes 147456
  33.6 46.3 %copy-start.9 = (bf16[1,1,256,32]{2,3,1,0:T(8,128)(2,1)S(1)}, bf16[1,1,256,32]{2,3,1,0:T(8,128)(2,1)}, u32[]{:S(2)}) copy-start(bf16[1,1,256,32]{2,3,1,0:T(8,128)(2,1)} %param.21) | copy-start | bytes 49156
  33.6 46.2 %copy-start.10 = (f32[1,1,256]{2,1,0:T(1,128)S(1)}, f32[1,1,256]{2,1,0:T(1,128)}, u32[]{:S(2)}) copy-start(f32[1,1,256]{2,1,0:T(1,128)} %param.19) | copy-start | bytes 3076
  81.6 0.7 copy-start.6
  89.4 4.5 copy-start.2
  109.8 0.6 copy-start.15
  116.4 176.8 %reduce-scatter.17.cloned.1.call-start = ((), (), s32[]{:S(2)}) async-start(), calls=%async_computation.6 | async-start | bytes 147456
  119.0 70.2 %copy-start.11 = (f32[1,1,256]{2,1,0:T(1,128)S(1)}, f32[1,1,256]{2,1,0:T(1,128)}, u32[]{:S(2)}) copy-start(f32[1,1,256]{2,1,0:T(1,128)} %param.19) | copy-start | bytes 3076
  190.9 0.6 copy-start.7
  198.4 4.5 copy-start.3
  198.4 4.6 copy-start.16
  223.6 167.2 %reduce-scatter.19.cloned.1.call-start = ((), (), s32[]{:S(2)}) async-start(), calls=%async_computation.7 | async-start | bytes 147456
  226.1 67.1 %copy-start.12 = (f32[1,1,256]{2,1,0:T(1,128)S(1)}, f32[1,1,256]{2,1,0:T(1,128)}, u32[]{:S(2)}) copy-start(f32[1,1,256]{2,1,0:T(1,128)} %param.19) | copy-start | bytes 3076
  294.4 6.5 %copy-start.8 = (bf16[256,256]{1,0:T(8,128)(2,1)}, bf16[256,256]{1,0:T(8,128)(2,1)S(1)}, u32[]{:S(2)}) copy-start(bf16[256,256]{1,0:T(8,128)(2,1)S(1)} %get-tuple-element.189) | copy-start | bytes 393220
  300.9 0.8 copy-start.5
  305.2 4.5 copy-start.17
  309.7 145.9 %copy-start.13 = (f32[256]{0:T(256)S(1)}, f32[256]{0:T(256)}, u32[]{:S(2)}) copy-start(f32[256]{0:T(256)} %reduce_sum.73) | copy-start | bytes 3076
Sparse Core Ops, SparseCore 0:
  15.3 64.5 reduce-scatter.12
  116.5 60.1 reduce-scatter.14
  223.7 58.4 reduce-scatter.16
  305.3 60.5 reduce-scatter.18
